TPU v7x, 256 devices: a whole 4x4x8 slice. The times are simulated.
256 devices in a mesh: row: 16 (over x, z_hi), col: 8 (over y, core), ga: 2 (over z_lo).
Axes of the slice: x: 4, y: 4, z: 8 (z_hi: 4, z_lo: 2; z = z_hi * 2 + z_lo), core: 2. Of those that a mesh axis runs over, the one named last changes fastest.
Arguments:
- pair_density: float32 [512, 24, 3072], P('row', None, 'ga'), may hold values from -6 to 6
- coulomb: float32 [3072], P('ga'), may hold values from 0.1 to 2
Outputs:
- kernel: float32 [12288, 12288], P('row', 'col')
All inputs are finite; a program needn't handle non-finite values.
Results may differ from a plain program's by a relative error of at most 0.00011.
Values sent between devices are 32-bit elements; how exact they have to be, the bound alone decides.
A program may use at most 64 MiB of HBM per device.

v0:
```python
import jax
import jax.numpy as jnp
from jax import lax
from jax.sharding import PartitionSpec as P


def rows_for(lines, peers):
    spare = -lines.shape[0] % peers
    if not spare:
        return lines
    return jnp.concatenate([lines, jnp.zeros((spare, *lines.shape[1:]), lines.dtype)])


def from_root(value, axis, root):
    lines = jnp.where(lax.axis_index(axis) == root, value, jnp.zeros_like(value)).reshape(
        -1, *value.shape[1:][-1:]
    )
    padded = rows_for(lines, lax.axis_size(axis))
    own = lax.psum_scatter(padded, axis, scatter_dimension=0, tiled=True)
    return lax.all_gather(own, axis, axis=0, tiled=True)[: len(lines)].reshape(value.shape)


def sent_to_all(value, axis):
    copies = jnp.broadcast_to(value, (lax.axis_size(axis), *value.shape))
    return lax.all_to_all(copies, axis, split_axis=0, concat_axis=0, tiled=True)


def taken_together(value, axis):
    return sent_to_all(value, axis).sum(axis=0)


def contract(left_rows, right_rows):
    return lax.dot_general(
        left_rows,
        right_rows,
        (((1,), (1,)), ((), ())),
        precision=lax.Precision.HIGHEST,
        preferred_element_type=jnp.float32,
    )


def local(pair_density, coulomb):
    row_count = lax.axis_size("row")
    col_count = lax.axis_size("col")
    here_row = lax.axis_index("row")
    here_col = lax.axis_index("col")
    doubled = 2.0 * coulomb
    local_k, bands, g_width = pair_density.shape
    grouped = pair_density.reshape(local_k // col_count, col_count, bands, g_width)
    own_columns = lax.dynamic_index_in_dim(grouped, here_col, 1, keepdims=False)
    columns = lax.all_gather(own_columns, "row", axis=0, tiled=True)
    ratio = row_count // col_count
    chosen = lax.dynamic_index_in_dim(
        columns.reshape(local_k, ratio, bands, g_width), here_row // col_count, 1, keepdims=False
    )
    rows_data = from_root(chosen, "col", here_row % col_count)
    weighted = rows_data.reshape(local_k * bands, g_width) * doubled[None, :]
    partial_value = contract(weighted, columns.reshape(columns.shape[0] * bands, g_width))
    summed = taken_together(partial_value, "ga")
    total_k = local_k * row_count
    return summed / jnp.float32(total_k)


def solution(mesh):
    placed = (P("row", None, "ga"), P("ga"))
    return jax.shard_map(
        local, mesh=mesh, in_specs=placed, out_specs=P("row", "col"), check_vma=False
    )
```

profile of v0, /device:TPU:1, one launch (start us, length us, event | category | flops | bytes accessed | tf_op | source)
XLA Modules:
  0.0 380.6 jit_solution(15559402277794939784)
XLA Ops:
  6.5 0.0 all-gather.6.cloned.1.call-start
  6.5 1.9 constant_dynamic-slice_fusion
  8.5 0.0 all-gather.6.cloned.1.call-update
  8.5 0.0 reduce-scatter.2.cloned.1.call-start
  8.6 125.7 %all-gather.6.cloned.1.call-done = f32[64,1,24,1536]{3,2,1,0:T(8,128)} async-done(((f32[4,1,24,1536]{3,2,1,0:T(8,128)}), f32[64,1,24,1536]{3,2,1,0:T(8,128)}) %all-gather.6.cloned.1.call-update) | async-done | bytes 9437200 | tf_op jit(solution)/shard_map/all_gather | solution.py:51
  134.3 5.0 %dynamic-slice_select_fusion = f32[32,1,24,1536]{3,2,1,0:T(8,128)} fusion(f32[32,2,24,1536]{3,2,1,0:T(8,128)} %bitcast.6, s32[]{:T(128)S(6)} %select_n.35, pred[]{:T(512)S(6)} %eq.5), kind=kLoop, calls=%fused_computation.2 | loop fusion | flops 1179648 | bytes 9437189 | tf_op jit(solution)/shard_map/jit(_where)/select_n | solution.py:15
  139.3 0.0 copy-start
  139.3 0.0 reduce-scatter.2.cloned.1.call-update
  139.3 0.0 all-gather.4.cloned.1.call-start
  139.3 44.3 %reduce-scatter.2.cloned.1.call-done = f32[96,1536]{1,0:T(8,128)} async-done(((f32[768,1536]{1,0:T(8,128)}), f32[96,1536]{1,0:T(8,128)}) %reduce-scatter.2.cloned.1.call-update) | async-done | bytes 589840 | tf_op jit(solution)/shard_map/reduce_scatter | solution.py:19
  183.7 0.0 all-gather.4.cloned.1.call-update
  183.7 0.0 copy-done
  183.7 40.9 %all-gather.4.cloned.1.call-done = f32[768,1536]{1,0:T(8,128)} async-done(((f32[96,1536]{1,0:T(8,128)}), f32[768,1536]{1,0:T(8,128)}) %all-gather.4.cloned.1.call-update) | async-done | bytes 4718608 | tf_op jit(solution)/shard_map/all_gather | solution.py:20
  224.7 28.0 %fusion = f32[768,1536]{1,0:T(8,128)S(1)} fusion(f32[1536,1536]{1,0:T(8,128)} %bitcast.7, f32[768,1536]{1,0:T(8,128)} %all-gather.4.cloned.1.call-done, f32[1536]{0:T(1024)S(1)} %broadcast_multiply_fusion.1), kind=kOutput, calls=%fused_computation | convolution fusion | flops 21744451584 | bytes 18880512 | tf_op jit(solution)/shard_map/dot_general | solution.py:33
  252.7 1.2 broadcast_in_dim.8
  253.9 107.9 %all_to_all.5 = f32[2,768,1536]{2,1,0:T(8,128)} all-to-all(f32[2,768,1536]{2,1,0:T(8,128)S(1)} %broadcast_in_dim.8), channel_id=1, replica_groups=mesh['row'=16,'col'=8,'ga'=2] {'ga'}, dimensions={0} | all-to-all | bytes 18874368 | tf_op jit(solution)/shard_map/all_to_all | solution.py:25
  361.8 7.3 %reduce_sum.9 = f32[768,1536]{1,0:T(8,128)} reduce(f32[2,768,1536]{2,1,0:T(8,128)} %all_to_all.5, f32[]{:T(128)} %constant.51.clone.1), dimensions={0}, to_apply=%region_1.2 | reduce | flops 1179648 | bytes 14155780 | tf_op jit(solution)/shard_map/reduce_sum | solution.py:29
  369.1 5.0 %broadcast_multiply_fusion = f32[768,1536]{1,0:T(8,128)} fusion(f32[768,1536]{1,0:T(8,128)} %reduce_sum.9), kind=kLoop, calls=%fused_computation.3 | loop fusion | flops 1179648 | bytes 9437184 | tf_op jit(solution)/shard_map/div | solution.py:61
  (1 shorter events, 0.0 us)
Async XLA Ops:
  6.5 127.7 %all-gather.6.cloned.1.call-start = ((), (), s32[]{:S(2)}) async-start(), calls=%async_computation.4 | async-start | bytes 10027008 | tf_op jit(solution)/shard_map/all_gather | solution.py:51
  8.5 175.2 %reduce-scatter.2.cloned.1.call-start = ((), (), s32[]{:S(2)}) async-start(), calls=%async_computation.2 | async-start | bytes 5308416 | tf_op jit(solution)/shard_map/reduce_scatter | solution.py:19
  139.3 44.4 %copy-start = (f32[1536]{0:T(1024)S(1)}, f32[1536]{0:T(1024)}, u32[]{:S(2)}) copy-start(f32[1536]{0:T(1024)} %param.3) | copy-start | bytes 18436
  139.3 85.4 %all-gather.4.cloned.1.call-start = ((), (), s32[]{:S(2)}) async-start(), calls=%async_computation.3 | async-start | bytes 5308416 | tf_op jit(solution)/shard_map/all_gather | solution.py:20
Sparse Core Ops, SparseCore 0:
  9.8 124.4 all-gather.5
  139.4 44.2 reduce-scatter.1
  185.5 39.1 all-gather.3
where the time goes:
time: 381 us
  waiting for transfers between devices  211 us (55%)
  blocking collectives  108 us (28%)
  matrix products  28 us (7%)
  other arithmetic  17.3 us (5%)
  between operations  13.2 us (3%)
    all_gather x1, waiting for transfers between devices, local(): columns = lax.all_gather(own_columns, 'row', axis=0, tiled=True)  126 us
    all_to_all x1, blocking collectives, sent_to_all(): return lax.all_to_all(copies, axis, split_axis=0, concat_axis=0, tiled=True)  108 us
    reduce_scatter x1, waiting for transfers between devices, from_root(): own = lax.psum_scatter(padded, axis, scatter_dimension=0, tiled=True)  44.3 us
    all_gather x1, waiting for transfers between devices, from_root(): lax.all_gather(own, axis, axis=0, tiled=True)[:len(lines)]  40.9 us
    dot_general x1, matrix products, contract(): lax.dot_general(left_rows, right_rows, (((1,), (1,)), ((), ())), precisio...  28 us
  transfers between devices with their start and end apart: 3, of which 3 were waited for; matrix products, arithmetic and copies ran while one was open for 0% of the time, Pallas kernels for 0%

commit v1 on v0

--- a/solution.py
+++ b/solution.py
@@ -48,7 +48,16 @@
     local_k, bands, g_width = pair_density.shape
     grouped = pair_density.reshape(local_k // col_count, col_count, bands, g_width)
     own_columns = lax.dynamic_index_in_dim(grouped, here_col, 1, keepdims=False)
-    columns = lax.all_gather(own_columns, "row", axis=0, tiled=True)
+    point_terms = lambda local_block: jnp.concatenate(
+        lax.all_to_all(
+            jnp.stack([local_block for _ in range(lax.axis_size("row"))], 0),
+            concat_axis=0,
+            split_axis=0,
+            axis_name="row",
+        ),
+        0,
+    )
+    columns = point_terms(own_columns)
     ratio = row_count // col_count
     chosen = lax.dynamic_index_in_dim(
         columns.reshape(local_k, ratio, bands, g_width), here_row // col_count, 1, keepdims=False

time: 381 us -> 487 us (1.28)
  waiting for transfers between devices: 211 us -> 301 us
  starting transfers between devices: 0.09 us -> 11.7 us
    all_to_all x0 -> x1, waiting for transfers between devices: none -> 212 us  [local(): lax.all_to_all(jnp.stack([local_block for _ in range(lax.axis_size('row')...]
    all_gather x1 -> x0, waiting for transfers between devices: 126 us -> none  [local(): columns = lax.all_gather(own_columns, 'row', axis=0, tiled=True)]
    all_to_all x0 -> x1, starting transfers between devices: none -> 11.6 us  [local(): lax.all_to_all(jnp.stack([local_block for _ in range(lax.axis_size('row')...]
    another operation x0 -> x2, local copies, waits for them, and re-layouts: none -> 5.96 us  [local(): jnp.stack([local_block for _ in range(lax.axis_size('row'))], 0)]
where the time goes in v1:
time: 487 us
  waiting for transfers between devices  301 us (62%)
  blocking collectives  108 us (22%)
  matrix products  28 us (6%)
  other arithmetic  17.3 us (4%)
  between operations  13.5 us (3%)
  starting transfers between devices  11.7 us (2%)
  local copies, waits for them, and re-layouts  7.19 us (1%)
    all_to_all x1, waiting for transfers between devices, local(): lax.all_to_all(jnp.stack([local_block for _ in range(lax.axis_size('row')...  212 us
    all_to_all x1, blocking collectives, sent_to_all(): return lax.all_to_all(copies, axis, split_axis=0, concat_axis=0, tiled=True)  108 us
    reduce_scatter x1, waiting for transfers between devices, from_root(): own = lax.psum_scatter(padded, axis, scatter_dimension=0, tiled=True)  48.5 us
    all_gather x1, waiting for transfers between devices, from_root(): lax.all_gather(own, axis, axis=0, tiled=True)[:len(lines)]  40.9 us
    dot_general x1, matrix products, contract(): lax.dot_general(left_rows, right_rows, (((1,), (1,)), ((), ())), precisio...  28 us
    all_to_all x1, starting transfers between devices, local(): lax.all_to_all(jnp.stack([local_block for _ in range(lax.axis_size('row')...  11.6 us
  transfers between devices with their start and end apart: 3, of which 3 were waited for; matrix products, arithmetic and copies ran while one was open for 0% of the time, Pallas kernels for 0%

profile of v1, /device:TPU:1, one launch (start us, length us, event | category | flops | bytes accessed | tf_op | source)
XLA Modules:
  0.0 486.7 jit_solution(8287528157460049204)
XLA Ops:
  6.5 1.1 dynamic-slice_bitcast_fusion
  7.6 4.9 stack.5
  12.5 11.6 %all-to-all-start = ((f32[16,4,24,1536]{3,2,1,0:T(8,128)}), f32[16,4,24,1536]{3,2,1,0:T(8,128)}, u32[]{:S(2)}, u32[]{:S(2)}) async-start(f32[16,4,24,1536]{3,2,1,0:T(8,128)} %stack.5), calls=%async_computation | async-start | bytes 18874368 | tf_op jit(solution)/shard_map/all_to_all | solution.py:52
  24.1 0.0 reduce-scatter.2.cloned.1.call-start
  24.2 211.7 %all-to-all-done = f32[16,4,24,1536]{3,2,1,0:T(8,128)} async-done(((f32[16,4,24,1536]{3,2,1,0:T(8,128)}), f32[16,4,24,1536]{3,2,1,0:T(8,128)}, u32[]{:S(2)}, u32[]{:S(2)}) %all-to-all-start) | async-done | bytes 9437216 | tf_op jit(solution)/shard_map/all_to_all | solution.py:52
  235.9 5.0 %dynamic-slice_select_fusion = f32[32,1,24,1536]{3,2,1,0:T(8,128)} fusion(f32[32,2,24,1536]{3,2,1,0:T(8,128)} %bitcast.2, s32[]{:T(128)S(6)} %select_n.35, pred[]{:T(512)S(6)} %eq.5), kind=kLoop, calls=%fused_computation.2 | loop fusion | flops 1179648 | bytes 9437189 | tf_op jit(solution)/shard_map/jit(_where)/select_n | solution.py:15
  240.9 0.0 copy-start
  240.9 0.0 reduce-scatter.2.cloned.1.call-update
  240.9 0.0 all-gather.2.cloned.1.call-start
  240.9 48.5 %reduce-scatter.2.cloned.1.call-done = f32[96,1536]{1,0:T(8,128)} async-done(((f32[768,1536]{1,0:T(8,128)}), f32[96,1536]{1,0:T(8,128)}) %reduce-scatter.2.cloned.1.call-update) | async-done | bytes 589840 | tf_op jit(solution)/shard_map/reduce_scatter | solution.py:19
  289.5 0.0 all-gather.2.cloned.1.call-update
  289.5 0.0 copy-done
  289.5 40.9 %all-gather.2.cloned.1.call-done = f32[768,1536]{1,0:T(8,128)} async-done(((f32[96,1536]{1,0:T(8,128)}), f32[768,1536]{1,0:T(8,128)}) %all-gather.2.cloned.1.call-update) | async-done | bytes 4718608 | tf_op jit(solution)/shard_map/all_gather | solution.py:20
  330.4 28.0 %fusion = f32[768,1536]{1,0:T(8,128)S(1)} fusion(f32[1536,1536]{1,0:T(8,128)} %bitcast.4, f32[768,1536]{1,0:T(8,128)} %all-gather.2.cloned.1.call-done, f32[1536]{0:T(1024)S(1)} %broadcast_multiply_fusion.1), kind=kOutput, calls=%fused_computation | convolution fusion | flops 21744451584 | bytes 18880512 | tf_op jit(solution)/shard_map/dot_general | solution.py:33
  358.5 1.2 broadcast_in_dim.8
  359.7 107.9 %all_to_all.10 = f32[2,768,1536]{2,1,0:T(8,128)} all-to-all(f32[2,768,1536]{2,1,0:T(8,128)S(1)} %broadcast_in_dim.8), channel_id=1, replica_groups=mesh['row'=16,'col'=8,'ga'=2] {'ga'}, dimensions={0} | all-to-all | bytes 18874368 | tf_op jit(solution)/shard_map/all_to_all | solution.py:25
  467.5 7.3 %reduce_sum.9 = f32[768,1536]{1,0:T(8,128)} reduce(f32[2,768,1536]{2,1,0:T(8,128)} %all_to_all.10, f32[]{:T(128)} %constant.51.clone.1), dimensions={0}, to_apply=%region_1.2 | reduce | flops 1179648 | bytes 14155780 | tf_op jit(solution)/shard_map/reduce_sum | solution.py:29
  474.8 5.0 %broadcast_multiply_fusion = f32[768,1536]{1,0:T(8,128)} fusion(f32[768,1536]{1,0:T(8,128)} %reduce_sum.9), kind=kLoop, calls=%fused_computation.3 | loop fusion | flops 1179648 | bytes 9437184 | tf_op jit(solution)/shard_map/div | solution.py:70
  (1 shorter events, 0.0 us)
Async XLA Ops:
  12.5 223.4 %all-to-all-start = ((f32[16,4,24,1536]{3,2,1,0:T(8,128)}), f32[16,4,24,1536]{3,2,1,0:T(8,128)}, u32[]{:S(2)}, u32[]{:S(2)}) async-start(f32[16,4,24,1536]{3,2,1,0:T(8,128)} %stack.5), calls=%async_computation | async-start | bytes 18874368 | tf_op jit(solution)/shard_map/all_to_all | solution.py:52
  24.1 265.4 %reduce-scatter.2.cloned.1.call-start = ((), (), s32[]{:S(2)}) async-start(), calls=%async_computation.3 | async-start | bytes 5308416 | tf_op jit(solution)/shard_map/reduce_scatter | solution.py:19
  240.9 48.6 %copy-start = (f32[1536]{0:T(1024)S(1)}, f32[1536]{0:T(1024)}, u32[]{:S(2)}) copy-start(f32[1536]{0:T(1024)} %param.3) | copy-start | bytes 18436
  240.9 89.5 %all-gather.2.cloned.1.call-start = ((), (), s32[]{:S(2)}) async-start(), calls=%async_computation.4 | async-start | bytes 5308416 | tf_op jit(solution)/shard_map/all_gather | solution.py:20
Sparse Core Ops, SparseCore 0:
  241.0 48.4 reduce-scatter.1
  291.3 39.0 all-gather.1
